TPU v7x, 32 devices: a 4x2x2 block of a 4x4x8 slice. The times are simulated.
32 devices in a mesh: dp: 4 (over y, z), tp: 8 (over x, core).
Axes of the slice: x: 4, y: 2, z: 2, core: 2. Of those that a mesh axis runs over, the one named last changes fastest.
The devices are a block of a 4x4x8 slice.
Arguments:
- x_a: bfloat16 [2048, 3072], P(('dp', 'tp')), parts along dimension 0
- x_b: bfloat16 [2048, 3072], P(('dp', 'tp')), parts along dimension 0
- labels_a: int32 [2048], P(('dp', 'tp')), parts along dimension 0
- labels_b: int32 [2048], P(('dp', 'tp')), parts along dimension 0
- w_head: bfloat16 [3072, 49152], P(None, 'tp')
Outputs:
- output 1: float32 [8], P('dp'), parts along dimension 0
- output 2: bfloat16 [12288, 49152], P('dp', 'tp'), parts along dimension 0
- output 3: bfloat16 [2048, 3072], P(('dp', 'tp')), parts along dimension 0
- output 4: bfloat16 [2048, 3072], P(('dp', 'tp')), parts along dimension 0
There are 4 independent parts. A program takes and returns all parts, laid end to end along the dimension named above; an argument that names none is the same for every part.
All inputs are finite; a program needn't handle non-finite values.
Results may differ from a plain program's by a relative error of at most 0.001.
Values are sent between devices in bfloat16 or wider.
A program may use at most 768 MiB of HBM per device.

v0:
```python
import jax
import jax.numpy as jnp
from jax import lax
from jax.sharding import PartitionSpec as P


def solution(mesh):
    group_size = mesh.shape["tp"]

    def local_step(x_a, x_b, labels_a, labels_b, w_local):
        tok_rows = x_a.shape[0]
        shard_cols = w_local.shape[1]
        tokens = tok_rows * group_size
        x_full = lax.all_gather(jnp.stack([x_a, x_b]), "tp", axis=1, tiled=True)
        label_full = lax.all_gather(jnp.stack([labels_a, labels_b]), "tp", axis=1, tiled=True)
        logits = jnp.einsum("mth,hv->mtv", x_full, w_local, preferred_element_type=jnp.float32)
        col_ids = lax.broadcasted_iota(jnp.int32, (1, 1, shard_cols), 2) + lax.axis_index("tp") * shard_cols
        label_hit = col_ids == label_full[..., None]
        local_target = jnp.sum(jnp.where(label_hit, logits, 0.0), axis=-1)
        row_max = lax.pmax(jnp.max(logits, axis=-1), "tp")
        shifted = jnp.exp(logits - row_max[..., None])
        stat_sums = lax.psum(jnp.stack([jnp.sum(shifted, axis=-1), local_target]), "tp")
        row_sum = stat_sums[0]
        loss_tok = row_max + jnp.log(row_sum) - stat_sums[1]
        losses = jnp.mean(loss_tok, axis=-1)
        grad_logits = ((shifted / row_sum[..., None] - label_hit.astype(jnp.float32)) / tokens).astype(jnp.bfloat16)
        grad_w = jnp.einsum("mth,mtv->hv", x_full, grad_logits, preferred_element_type=jnp.float32).astype(jnp.bfloat16)
        grad_part = jnp.einsum("mtv,hv->mth", grad_logits, w_local, preferred_element_type=jnp.float32)
        grad_x = lax.psum_scatter(grad_part, "tp", scatter_dimension=1, tiled=True).astype(jnp.bfloat16)
        return losses, grad_w, grad_x[0], grad_x[1]

    row_spec = P(("dp", "tp"), None)
    label_spec = P(("dp", "tp"))
    return jax.shard_map(local_step, mesh=mesh, in_specs=(row_spec, row_spec, label_spec, label_spec, P(None, "tp")), out_specs=(P("dp"), P("dp", "tp"), row_spec, row_spec), check_vma=False)
```

profile of v0, /device:TPU:81, one launch (start us, length us, event | category | flops | bytes accessed | tf_op | source)
XLA Modules:
  0.0 278.0 jit_solution(14233245910433167833)
XLA Ops:
  7.2 0.1 all-gather.3.cloned.1.call-start
  7.2 2.1 pad_maximum_fusion
  9.3 0.1 all-gather.3.cloned.1.call-update
  9.4 0.1 reduce-scatter.2.cloned.1.call-start
  9.5 0.7 add_bitcast_fusion
  10.1 12.3 %all-gather = s32[8,64,2]{1,2,0:T(2,128)S(1)} all-gather(s32[1,64,2]{1,2,0:T(2,128)S(1)} %add_bitcast_fusion), channel_id=1, replica_groups=mesh['dp'=4,'tp'=8] {'tp'}, dimensions={0}, use_global_device_ids=true | all-gather | bytes 4608 | tf_op jit(solution)/shard_map/all_gather | solution.py:15
  22.4 0.1 reshape.17
  22.5 29.8 %all-gather.3.cloned.1.call-done = bf16[2,512,3072]{2,1,0:T(8,128)(2,1)} async-done(((bf16[2,64,3072]{2,1,0:T(8,128)(2,1)}), bf16[2,512,3072]{2,1,0:T(8,128)(2,1)}) %all-gather.3.cloned.1.call-update) | async-done | bytes 6291472 | tf_op jit(solution)/shard_map/all_gather | solution.py:14
  52.3 46.9 %fusion.13 = (f32[2,512]{1,0:T(2,128)S(1)}, f32[2,512,6144]{2,1,0:T(8,128)}) fusion(bf16[2,512,3072]{2,1,0:T(8,128)(2,1)} %all-gather.3.cloned.1.call-done, bf16[3072,6144]{1,0:T(8,128)(2,1)} %param.9), kind=kOutput, calls=%fused_computation.24 | convolution fusion | flops 38660997120 | bytes 69210112 | tf_op jit(solution)/shard_map/mth,hv->mtv/dot_general | solution.py:16
  99.2 12.0 %pmax.7 = f32[2,512]{1,0:T(2,128)S(1)} all-reduce(f32[2,512]{1,0:T(2,128)S(1)} %get-tuple-element.8), channel_id=1, replica_groups=mesh['dp'=4,'tp'=8] {'tp'}, use_global_device_ids=true, to_apply=%region_1.2 | all-reduce | flops 1024 | bytes 8192 | tf_op jit(solution)/shard_map/pmax | solution.py:20
  111.2 11.7 %fusion.8 = (f32[2,512]{1,0:T(2,128)S(1)}, f32[2,512]{1,0:T(2,128)S(1)}) fusion(f32[2,512,6144]{2,1,0:T(8,128)} %get-tuple-element.9, f32[2,512]{1,0:T(2,128)S(1)} %pmax.7, s32[2,512]{1,0:T(2,128)S(1)} %bitcast.44, s32[6144]{0:T(1024)S(1)} %iota_add_fusion), kind=kLoop, calls=%fused_computation.12 | loop fusion | flops 31455232 | bytes 25206784 | tf_op jit(solution)/shard_map/reduce_sum | solution.py:22
  122.9 13.5 %psum.7 = f32[2,2,512]{2,1,0:T(2,128)S(1)} all-reduce(f32[2,2,512]{2,1,0:T(2,128)S(1)} %pad_maximum_fusion.1), channel_id=1, replica_groups=mesh['dp'=4,'tp'=8] {'tp'}, use_global_device_ids=true, to_apply=%region_4.5 | all-reduce | flops 2048 | bytes 16384 | tf_op jit(solution)/shard_map/psum | solution.py:22
  136.5 16.2 %fusion.22 = bf16[2,512,6144]{2,1,0:T(8,128)(2,1)} fusion(f32[2,512,6144]{2,1,0:T(8,128)} %get-tuple-element.9, f32[2,512]{1,0:T(2,128)S(1)} %slice_bitcast_fusion.3, s32[2,512]{1,0:T(2,128)S(1)} %bitcast.45, s32[6144]{0:T(1024)S(1)} %iota_add_fusion, f32[2,512]{1,0:T(2,128)S(1)} %pmax.7), kind=kLoop, calls=%fused_computation.10.clone.clone.1 | loop fusion | flops 44040192 | bytes 37785600 | tf_op jit(solution)/shard_map/mtv,hv->mth/dot_general | solution.py:28
  152.7 47.9 %fusion = f32[2,512,3072]{2,1,0:T(8,128)} fusion(bf16[3072,6144]{1,0:T(8,128)(2,1)} %param.9, bf16[2,512,6144]{2,1,0:T(8,128)(2,1)} %fusion.22), kind=kOutput, calls=%fused_computation.1 | convolution fusion | flops 38654705664 | bytes 62914560 | tf_op jit(solution)/shard_map/mtv,hv->mth/dot_general | solution.py:28
  200.6 0.1 reduce-scatter.2.cloned.1.call-update
  200.7 0.1 fusion.10
  200.8 0.5 broadcast_multiply_fusion
  201.3 51.1 %bitcast_convert_fusion = bf16[3072,6144]{1,0:T(8,128)(2,1)} fusion(bf16[2,512,3072]{2,1,0:T(8,128)(2,1)} %all-gather.3.cloned.1.call-done, f32[2,512,6144]{2,1,0:T(8,128)} %get-tuple-element.9, f32[2,512]{1,0:T(2,128)S(1)} %slice_bitcast_fusion.3, s32[2,512]{1,0:T(2,128)S(1)} %bitcast.46, s32[6144]{0:T(1024)S(1)} %iota_add_fusion, f32[2,512]{1,0:T(2,128)S(1)} %pmax.7), kind=kOutput, calls=%fused_computation | convolution fusion | flops 38717620224 | bytes 69242880 | tf_op jit(solution)/shard_map/mth,mtv->hv/dot_general | solution.py:27
  252.4 16.2 %reduce-scatter.2.cloned.1.call-done = f32[2,64,3072]{2,1,0:T(8,128)} async-done(((f32[2,512,3072]{2,1,0:T(8,128)}), f32[2,64,3072]{2,1,0:T(8,128)}) %reduce-scatter.2.cloned.1.call-update) | async-done | bytes 1572880 | tf_op jit(solution)/shard_map/reduce_scatter | solution.py:29
  268.7 1.5 convert_element_type.15
  270.2 0.9 slice_bitcast_fusion
  (4 shorter events, 0.0 us)
Async XLA Ops:
  7.2 45.1 %all-gather.3.cloned.1.call-start = ((), (), s32[]{:S(2)}) async-start(), calls=%async_computation.1 | async-start | bytes 7077888 | tf_op jit(solution)/shard_map/all_gather | solution.py:14
  9.4 259.3 %reduce-scatter.2.cloned.1.call-start = ((), (), s32[]{:S(2)}) async-start(), calls=%async_computation.2 | async-start | bytes 14155776 | tf_op jit(solution)/shard_map/reduce_scatter | solution.py:29
Sparse Core Ops, SparseCore 0:
  10.2 42.0 all-gather.2
  200.8 67.8 reduce-scatter.1
where the time goes:
time: 278 us
  matrix products  146 us (53%)
  waiting for transfers between devices  46.1 us (17%)
  blocking collectives  37.8 us (14%)
  other arithmetic  32.8 us (12%)
  between operations  14.1 us (5%)
    dot_general x1, matrix products, local_step(): jnp.einsum('mth,mtv->hv', x_full, grad_logits, preferred_element_type=jnp...  51.1 us
    dot_general x1, matrix products, local_step(): jnp.einsum('mtv,hv->mth', grad_logits, w_local, preferred_element_type=jn...  47.9 us
    dot_general x1, matrix products, local_step(): jnp.einsum('mth,hv->mtv', x_full, w_local, preferred_element_type=jnp.flo...  46.9 us
    all_gather x1, waiting for transfers between devices, local_step(): x_full = lax.all_gather(jnp.stack([x_a, x_b]), 'tp', axis=1, tiled=True)  29.8 us
    reduce_scatter x1, waiting for transfers between devices, local_step(): lax.psum_scatter(grad_part, 'tp', scatter_dimension=1, tiled=True)  16.2 us
    dot_general x1, other arithmetic, local_step(): jnp.einsum('mtv,hv->mth', grad_logits, w_local, preferred_element_type=jn...  16.2 us
    psum x1, blocking collectives, local_step(): lax.psum(jnp.stack([jnp.sum(shifted, axis=-1), local_target]), 'tp')  13.5 us
    all_gather x1, blocking collectives, local_step(): lax.all_gather(jnp.stack([labels_a, labels_b]), 'tp', axis=1, tiled=True)  12.3 us
  transfers between devices with their start and end apart: 2, of which 2 were waited for; matrix products, arithmetic and copies ran while one was open for 19% of the time, Pallas kernels for 0%

commit v1 on v0

v1 whole, which is shorter than its diff:
```python
import functools
import jax
import jax.numpy as jnp
from jax import lax
from jax.experimental import pallas as pl
from jax.experimental.pallas import tpu as pltpu
from jax.sharding import PartitionSpec as P

MESH = pl.DeviceIdType.MESH
F32, BF16 = jnp.float32, jnp.bfloat16
NT = 512
NS = 6
LOW = -3.0e38
VMEM = 63 * 2**20


def peer(me, chips, dr, flip):
    chip, core = me // 2, me % 2
    other = (1 - core) if flip else core
    return lax.rem(chip + dr, chips) * 2 + other


def ring_peers(me, chips):
    return peer(me, chips, 1, False), peer(me, chips, chips - 1, False), peer(me, chips, 0, True)


def k1_kernel(n, xa, xb, lab, w, z_out, xt_out, lcol_out, lab_out, loss_out,
              xs, xc, ws, zb0, zb1, mc, sc, tc, lc, mm, ss, tt, labin, labrel, st, stin, lrow, lossb,
              wsem, zsem, lsem, xsend, xrecv, labsend, labrecv, stsend, strecv):
    me = lax.axis_index("tp")
    chips = n // 2
    tok = xa.shape[0]
    cols = w.shape[1]
    tiles = cols // NT
    per = tiles // NS
    wide = NT * NS
    rows = 4 * tok
    half = tok // 2
    right, left, partner = ring_peers(me, chips)
    others = [(dr, f) for dr in range(chips) for f in (False, True) if dr or f]
    lo, hi, both, far = pl.ds(0, tok), pl.ds(tok, tok), pl.ds(0, 2 * tok), pl.ds(2 * tok, 2 * tok)
    lo0, lo1 = pl.ds(0, half), pl.ds(half, half)

    def rcopy(src, dst, k, dev):
        return pltpu.make_async_remote_copy(src_ref=src, dst_ref=dst, send_sem=xsend.at[k],
                                            recv_sem=xrecv.at[k], device_id={"tp": dev}, device_id_type=MESH)

    def to_all(src, dst, send, recv):
        made = []
        for dr, f in others:
            slot = ((chips - dr) % chips) * 2 + int(f)
            made.append(pltpu.make_async_remote_copy(src_ref=src, dst_ref=dst(slot), send_sem=send.at[slot], recv_sem=recv.at[slot],
                                                     device_id={"tp": peer(me, chips, dr, f)}, device_id_type=MESH))
        return made

    wcopy = [pltpu.make_async_copy(w.at[:, pl.ds(j * wide, wide)], ws.at[:, pl.ds(j * wide, wide)], wsem.at[j]) for j in range(per)]
    la = pltpu.make_async_copy(xa, xs.at[0, lo], lsem.at[0])
    lb = pltpu.make_async_copy(xb, xs.at[0, hi], lsem.at[1])
    ll = pltpu.make_async_copy(lab, labin.at[0], lsem.at[2])
    la.start()
    lb.start()
    ll.start()
    for c in wcopy:
        c.start()

    barrier = pltpu.get_barrier_semaphore()
    for dr, f in others:
        pl.semaphore_signal(barrier, inc=1, device_id={"tp": peer(me, chips, dr, f)}, device_id_type=MESH)
    la.wait()
    lb.wait()
    ll.wait()
    pl.semaphore_wait(barrier, n - 1)

    own_a, own_b = xs.at[0, lo], xs.at[0, hi]
    c_p = rcopy(xs.at[0, both], xs.at[0, far], 0, partner)
    c_3a = rcopy(own_a, xs.at[1, hi], 1, right)
    c_1a = rcopy(own_a, xs.at[1, lo], 2, left)
    c_3b = rcopy(own_b, xs.at[2, hi], 3, right)
    c_1b = rcopy(own_b, xs.at[2, lo], 4, left)
    c_f3a = rcopy(xs.at[1, pl.ds(tok, half)], xs.at[3, lo0], 5, right)
    c_f1a = rcopy(xs.at[1, lo1], xs.at[3, lo1], 6, left)
    c_f3b = rcopy(xs.at[2, pl.ds(tok, half)], xs.at[3, pl.ds(tok, half)], 7, right)
    c_f1b = rcopy(xs.at[2, lo1], xs.at[3, pl.ds(tok + half, half)], 8, left)
    c_d = [None] + [rcopy(xs.at[g, both], xs.at[g, far], 8 + g, partner) for g in (1, 2, 3)]
    c_lab = to_all(labin.at[0], lambda slot: labin.at[slot], labsend, labrecv)
    for c in c_lab + [c_p, c_3a, c_1a, c_3b, c_1b]:
        c.start()

    lane = lax.broadcasted_iota(jnp.int32, (2 * tok, 128), 1)
    shift = me * cols

    def put_labels(slot):
        r, f = slot // 2, slot % 2
        t = jnp.broadcast_to(labin[slot, 0:1, :], (2 * tok, 128)).T - lane - shift
        at = f * 2 * tok
        if r in (0, 2):
            labrel[{0: 0, 2: 3}[r], at:at + 2 * tok] = t
        else:
            o = at + (0 if r == 1 else tok)
            labrel[1, o:o + tok] = t[:tok]
            labrel[2, o:o + tok] = t[tok:]

    put_labels(0)
    c_p.wait()
    for c in c_lab:
        c.wait()
    for slot in range(1, n):
        put_labels(slot)

    def z_copy(g, zb):
        q = 0 if zb is zb0 else 1
        return pltpu.make_async_copy(zb, z_out.at[g, q], zsem.at[q])

    def epilogue(z, base):
        for r0 in range(0, rows, 32):
            rs = pl.ds(r0, 32)
            zc = [z[rs, k * 128:(k + 1) * 128] for k in range(NT // 128)]
            m_old = mc[rs]
            lr = lc[rs]
            m_new = functools.reduce(jnp.maximum, zc, m_old)
            mc[rs] = m_new
            s = sc[rs] * jnp.exp(m_old - m_new)
            sc[rs] = s + functools.reduce(jnp.add, [jnp.exp(c - m_new) for c in zc])
            tc[rs] = tc[rs] + functools.reduce(jnp.add, [jnp.where(lr == base + k * 128, c, 0.0) for k, c in enumerate(zc)])

    def half_step(g, q, zb, zprev):
        for t in range(NS):
            if t:
                epilogue(zb.at[t - 1], (q * NS + t - 1) * NT)
            elif q:
                epilogue(zprev.at[NS - 1], (NS - 1) * NT)
            zb[t] = jnp.dot(xc[...], ws[:, (q * NS + t) * NT:(q * NS + t + 1) * NT], preferred_element_type=F32)

    def step(g, _):
        for ev, fn in events.items():
            if ev % 2 == 0:
                pl.when(g == ev // 2)(fn)
        xc[...] = xs[g]
        lc[...] = labrel[g]
        mc[...] = jnp.full((rows, 128), LOW, F32)
        sc[...] = jnp.zeros((rows, 128), F32)
        tc[...] = jnp.zeros((rows, 128), F32)

        @pl.when(g == 0)
        def _():
            wcopy[0].wait()

        @pl.when(g >= 1)
        def _():
            z_copy(g - 1, zb0).wait()

        half_step(g, 0, zb0, zb1)
        for ev, fn in events.items():
            if ev % 2 == 1:
                pl.when(g == ev // 2)(fn)

        @pl.when(g == 0)
        def _():
            wcopy[1].wait()

        @pl.when(g >= 1)
        def _():
            z_copy(g - 1, zb1).wait()

        z_copy(g, zb0).start()
        half_step(g, 1, zb1, zb0)
        z_copy(g, zb1).start()
        epilogue(zb1.at[NS - 1], (tiles - 1) * NT)
        mm[g] = mc[...]
        ss[g] = sc[...]
        tt[g] = tc[...]
        return 0

    def ev_a():
        c_3a.wait_recv()
        c_1a.wait_recv()
        c_d[1].start()
        c_f3a.start()
        c_f1a.start()

    def ev_a2():
        c_d[1].wait_recv()

    def ev_b():
        c_3b.wait_recv()
        c_1b.wait_recv()
        c_d[2].start()
        c_f3b.start()
        c_f1b.start()

    def ev_b2():
        c_d[2].wait_recv()

    def ev_f():
        for c in (c_f3a, c_f1a, c_f3b, c_f1b):
            c.wait_recv()
        c_d[3].start()

    def ev_f2():
        c_d[3].wait_recv()

    events = {1: ev_a, 2: ev_a2, 3: ev_b, 4: ev_b2, 5: ev_f, 6: ev_f2}
    lax.fori_loop(0, 4, step, 0)

    def rows_of(ref, r, f):
        at = f * 2 * tok
        if r in (0, 2):
            return ref[{0: 0, 2: 3}[r], at:at + 2 * tok]
        o = at + (0 if r == 1 else tok)
        return jnp.concatenate([ref[1, o:o + tok], ref[2, o:o + tok]], axis=0)

    for slot in range(n):
        r, f = slot // 2, slot % 2
        m, s, t = (rows_of(ref, r, f) for ref in (mm, ss, tt))
        m_row = jnp.max(m, axis=1, keepdims=True)
        s_row = jnp.sum(s * jnp.exp(m - m_row), axis=1, keepdims=True)
        t_row = jnp.sum(t, axis=1, keepdims=True)
        packed = jnp.where(lane == 0, m_row, jnp.where(lane == 1, s_row, t_row)).T
        row = peer(me, chips, r, bool(f))
        for k in range(3):
            st[k, pl.ds(row, 1)] = packed[k:k + 1]
    c_st = to_all(st, lambda slot: stin.at[me], stsend, strecv)
    for c in c_st:
        c.start()
    stin[me] = st[...]
    hid = xs.shape[2]
    def tr(h, _):
        hs = pl.ds(pl.multiple_of(h * 256, 256), 256)
        for g in range(4):
            ws[hs, g * rows:(g + 1) * rows] = xs[g, :, hs].T
        return 0
    lax.fori_loop(0, hid // 256, tr, 0)
    c_xt = pltpu.make_async_copy(ws.at[:, pl.ds(0, 4 * rows)], xt_out, lsem.at[0])
    c_xt.start()
    for c in c_st:
        c.wait()
    m_all = functools.reduce(jnp.maximum, [stin[d, 0] for d in range(n)])
    s_all = functools.reduce(jnp.add, [stin[d, 1] * jnp.exp(stin[d, 0] - m_all) for d in range(n)])
    t_all = functools.reduce(jnp.add, [stin[d, 2] for d in range(n)])
    lse = m_all + jnp.log(s_all)
    lrow[...] = lse
    tok_loss = lse - t_all
    la_s = jnp.sum(tok_loss[:, :tok], keepdims=True)
    lb_s = jnp.sum(tok_loss[:, tok:], keepdims=True)
    l2 = lax.broadcasted_iota(jnp.int32, (8, 128), 1)
    lossb[...] = jnp.where(l2 == 0, la_s, lb_s) * (1.0 / (tok * n))
    for slot in range(n):
        r, f = slot // 2, slot % 2
        row = peer(me, chips, r, bool(f))
        t = jnp.broadcast_to(lrow[pl.ds(row, 1)], (2 * tok, 128)).T
        at = f * 2 * tok
        if r in (0, 2):
            mm[{0: 0, 2: 3}[r], at:at + 2 * tok] = t
        else:
            o = at + (0 if r == 1 else tok)
            mm[1, o:o + tok] = t[:tok]
            mm[2, o:o + tok] = t[tok:]
    outs = [pltpu.make_async_copy(mm, lcol_out, lsem.at[1]), pltpu.make_async_copy(labrel, lab_out, lsem.at[2]),
            pltpu.make_async_copy(lossb, loss_out, lsem.at[3])]
    for c in outs:
        c.start()
    for c in outs:
        c.wait()
    c_xt.wait()
    z_copy(3, zb0).wait()
    z_copy(3, zb1).wait()
    for c in (c_3a, c_1a, c_3b, c_1b, c_f3a, c_f1a, c_f3b, c_f1b, c_d[1], c_d[2], c_d[3]):
        c.wait_send()


def k1(n, xa, xb, la, lb, w):
    tok, hid = xa.shape
    cols = w.shape[1]
    tiles = cols // NT
    rows = 4 * tok
    lab = jnp.broadcast_to(jnp.concatenate([la, lb])[None, :], (8, 2 * tok))
    any_ = pl.BlockSpec(memory_space=pltpu.MemorySpace.HBM)
    return pl.pallas_call(
        functools.partial(k1_kernel, n),
        out_shape=[jax.ShapeDtypeStruct((4, tiles // NS, NS, rows, NT), F32), jax.ShapeDtypeStruct((hid, 4 * rows), BF16),
                   jax.ShapeDtypeStruct((4, rows, 128), F32), jax.ShapeDtypeStruct((4, rows, 128), jnp.int32),
                   jax.ShapeDtypeStruct((8, 128), F32)],
        in_specs=[any_] * 4,
        out_specs=[any_] * 5,
        scratch_shapes=[
            pltpu.VMEM((4, rows, hid), BF16), pltpu.VMEM((rows, hid), BF16), pltpu.VMEM((hid, cols), BF16),
            pltpu.VMEM((NS, rows, NT), F32), pltpu.VMEM((NS, rows, NT), F32), pltpu.VMEM((rows, 128), F32), pltpu.VMEM((rows, 128), F32), pltpu.VMEM((rows, 128), F32), pltpu.VMEM((rows, 128), jnp.int32), pltpu.VMEM((4, rows, 128), F32), pltpu.VMEM((4, rows, 128), F32),
            pltpu.VMEM((4, rows, 128), F32), pltpu.VMEM((n, 8, 2 * tok), jnp.int32), pltpu.VMEM((4, rows, 128), jnp.int32),
            pltpu.VMEM((3, n, 2 * tok), F32), pltpu.VMEM((n, 3, n, 2 * tok), F32), pltpu.VMEM((n, 2 * tok), F32), pltpu.VMEM((8, 128), F32),
            pltpu.SemaphoreType.DMA((tiles // NS,)), pltpu.SemaphoreType.DMA((2,)), pltpu.SemaphoreType.DMA((4,)),
            pltpu.SemaphoreType.DMA((12,)), pltpu.SemaphoreType.DMA((12,)), pltpu.SemaphoreType.DMA((n,)), pltpu.SemaphoreType.DMA((n,)),
            pltpu.SemaphoreType.DMA((n,)), pltpu.SemaphoreType.DMA((n,)),
        ],
        compiler_params=pltpu.CompilerParams(collective_id=0, has_side_effects=True, vmem_limit_bytes=VMEM),
        name="gather_logits",
    )(xa, xb, lab, w)


HC = 512
ACCS = 3
PH, PC = 512, 1024


def k2_kernel(n, cover, z, lcol, lab, w, xt, dxa_out, dxb_out, g_out, dw_out,
              g, lv, bv, z4, w0, w1, xv, d0, d1, pr, acc, r1, r2, ob0, ob1, oa,
              zsem, wsem, lsem, gsem, osem, psend, precv, s1send, s1recv, s2send, s2recv, fsem):
    me = lax.axis_index("tp")
    chips = n // 2
    right, left, partner = ring_peers(me, chips)
    rows = z.shape[3]
    tok = rows // 4
    halves, sub = z.shape[1], z.shape[2]
    hid, cols = w.shape
    chunks = hid // HC
    zn = 4 * halves * sub // 3
    barrier = pltpu.get_barrier_semaphore()
    for dev in (right, left, partner):
        pl.semaphore_signal(barrier, inc=1, device_id={"tp": dev}, device_id_type=MESH)

    def z_load(i, slot):
        gi, rest = i // (halves * sub // 3), lax.rem(i, halves * sub // 3)
        q, t = rest // (sub // 3), lax.rem(rest, sub // 3)
        return pltpu.make_async_copy(z.at[gi, q, pl.ds(t * 3, 3)], z4.at[slot], zsem.at[slot])

    def w_load(k, buf):
        return pltpu.make_async_copy(w.at[pl.ds(pl.multiple_of(k * HC, HC), HC)], buf, wsem.at[0 if buf is w0 else 1])

    small = [pltpu.make_async_copy(lcol, lv, lsem.at[0]), pltpu.make_async_copy(lab, bv, lsem.at[1]),
             pltpu.make_async_copy(xt.at[pl.ds(0, xv.shape[0])], xv, lsem.at[2])]
    small[0].start()
    small[1].start()
    for i in range(3):
        z_load(jnp.int32(i), i).start()
    w_load(0, w0).start()
    w_load(1, w1).start()
    small[2].start()
    small[0].wait()
    small[1].wait()
    inv = 1.0 / (tok * n)

    def soft(i, _):
        slot = lax.rem(i, 4)

        @pl.when(i + 3 < zn)
        def _():
            z_load(i + 3, lax.rem(i + 3, 4)).start()

        z_load(i, slot).wait()
        gi, rest = i // (halves * sub // 3), lax.rem(i, halves * sub // 3)
        for r0 in range(0, rows, 32):
            rs = pl.ds(r0, 32)
            lse = lv[gi, rs]
            lr = bv[gi, rs] - rest * (3 * NT)
            for t in range(3):
                out = []
                for k in range(NT // 128):
                    p = jnp.exp(z4[slot, t, rs, k * 128:(k + 1) * 128] - lse)
                    out.append((jnp.where(lr == t * NT + k * 128, p - 1.0, p) * inv).astype(BF16))
                g[pl.ds(pl.multiple_of(gi * rows + r0, 32), 32), pl.ds(pl.multiple_of(rest * (3 * NT) + t * NT, NT), NT)] = jnp.concatenate(out, axis=1)
        return 0

    lax.fori_loop(0, zn, soft, 0)
    c_g = pltpu.make_async_copy(g, g_out, gsem)
    c_g.start()
    small[2].wait()
    pl.semaphore_wait(barrier, 3)

    def remote(src, dst, ss, rs, dev):
        return pltpu.make_async_remote_copy(src_ref=src, dst_ref=dst, send_sem=ss, recv_sem=rs,
                                            device_id={"tp": dev}, device_id_type=MESH)

    lo, hi = pl.ds(0, tok), pl.ds(tok, tok)

    def pair(c, d):
        return remote(d.at[:, pl.ds(2 * tok, 2 * tok)], pr.at[c], psend.at[c], precv.at[c], partner)

    def first(c):
        a = acc.at[lax.rem(c, ACCS)]
        return [remote(a.at[3, lo], r1.at[c, 0], s1send.at[c, 0], s1recv.at[c, 0], right),
                remote(a.at[3, hi], r1.at[c, 1], s1send.at[c, 1], s1recv.at[c, 1], left),
                remote(a.at[2, lo], r2.at[c, 1], s2send.at[c, 1], s2recv.at[c, 1], right),
                remote(a.at[1, hi], r2.at[c, 2], s2send.at[c, 2], s2recv.at[c, 2], left)]

    def second(c):
        a = acc.at[lax.rem(c, ACCS)]
        return [remote(a.at[1, lo], r2.at[c, 0], s2send.at[c, 0], s2recv.at[c, 0], right),
                remote(a.at[2, hi], r2.at[c, 3], s2send.at[c, 3], s2recv.at[c, 3], left)]

    def do_first(c, d):
        pair(c, d).wait_recv()
        for b in range(4):
            acc[lax.rem(c, ACCS), b] = d[b, 0:2 * tok] + pr[c, b]
        for cp in first(c):
            cp.start()

    def do_second(c):
        f = first(c)
        f[0].wait_recv()
        f[1].wait_recv()
        s = lax.rem(c, ACCS)
        acc[s, 1, 0:tok] = acc[s, 1, 0:tok] + r1[c, 0]
        acc[s, 2, tok:] = acc[s, 2, tok:] + r1[c, 1]
        for cp in second(c):
            cp.start()

    def do_last(c):
        f, e = first(c), second(c)
        for cp in f[2:] + e:
            cp.wait_recv()
        s = lax.rem(c, ACCS)
        hs = pl.ds(pl.multiple_of(c * HC, HC), HC)
        oa[0:tok, hs] = (acc[s, 0, 0:tok] + (r2[c, 0] + r2[c, 2])).astype(BF16)
        oa[tok:, hs] = (acc[s, 0, tok:] + (r2[c, 1] + r2[c, 3])).astype(BF16)
        for cp in f + e:
            cp.wait_send()

    pcs = cols // PC

    def dw_copy(p, ob):
        hb, cb = p // pcs, lax.rem(p, pcs)
        return pltpu.make_async_copy(ob, dw_out.at[pl.ds(pl.multiple_of(hb * PH, PH), PH), pl.ds(pl.multiple_of(cb * PC, PC), PC)],
                                     osem.at[0 if ob is ob0 else 1])

    def dw_dot(p, ob):
        hb, cb = p // pcs, lax.rem(p, pcs)
        ob[...] = jnp.dot(xv[pl.ds(pl.multiple_of(hb * PH, PH), PH)], g[:, pl.ds(pl.multiple_of(cb * PC, PC), PC)],
                          preferred_element_type=F32).astype(BF16)

    obs = (ob0, ob1)

    def half(it, wb, d, dprev):
        w_load(it, wb).wait()

        @pl.when(it >= 2)
        def _():
            pair(it - 2, d).wait_send()

        d[...] = lax.dot_general(g[...], wb[...], (((1,), (1,)), ((), ())), preferred_element_type=F32).reshape(4, rows, HC)
        pair(it, d).start()

        @pl.when(it + 2 < chunks)
        def _():
            w_load(it + 2, wb).start()

        @pl.when(it >= 1)
        def _():
            do_second(it - 1)
            for i, ob in enumerate(obs):
                dw_copy(2 * it - 2 + i, ob).wait()

        for i, ob in enumerate(obs):
            dw_dot(2 * it + i, ob)
        for i, ob in enumerate(obs):
            dw_copy(2 * it + i, ob).start()
        do_first(it, d)

        @pl.when(it >= 2)
        def _():
            do_last(it - 2)

    def step(i2, _):
        half(2 * i2, w0, d0, d1)
        half(2 * i2 + 1, w1, d1, d0)
        return 0

    lax.fori_loop(0, chunks // 2, step, 0)
    end = jnp.int32(chunks - 1)

    def two(i, _):
        p = 2 * chunks + 2 * i
        for j, ob in enumerate(obs):
            dw_copy(p - 2 + j, ob).wait()
        for j, ob in enumerate(obs):
            dw_dot(p + j, ob)
        for j, ob in enumerate(obs):
            dw_copy(p + j, ob).start()

        @pl.when(i == 1)
        def _():
            do_second(end)
            do_last(end - 1)
        return 0

    lax.fori_loop(0, cover // 2 - chunks, two, 0)
    do_last(end)
    outs = [pltpu.make_async_copy(oa.at[lo], dxa_out, fsem.at[0]), pltpu.make_async_copy(oa.at[hi], dxb_out, fsem.at[1])]
    for c in outs:
        c.start()
    pair(chunks - 2, d0).wait_send()
    pair(chunks - 1, d1).wait_send()
    dw_copy(cover - 2, ob0).wait()
    dw_copy(cover - 1, ob1).wait()
    c_g.wait()
    for c in outs:
        c.wait()


def k2(n, cover, z, lcol, lab, w, xt):
    hid, cols = w.shape
    rows = z.shape[3]
    tok = rows // 4
    chunks = hid // HC
    part = cover // (cols // PC) * PH
    hbm = pl.BlockSpec(memory_space=pltpu.MemorySpace.HBM)
    dma = pltpu.SemaphoreType.DMA
    return pl.pallas_call(
        functools.partial(k2_kernel, n, cover),
        out_shape=[jax.ShapeDtypeStruct((tok, hid), BF16), jax.ShapeDtypeStruct((tok, hid), BF16),
                   jax.ShapeDtypeStruct((4 * rows, cols), BF16), jax.ShapeDtypeStruct((part, cols), BF16)],
        in_specs=[hbm] * 5,
        out_specs=[hbm] * 4,
        scratch_shapes=[
            pltpu.VMEM((4 * rows, cols), BF16), pltpu.VMEM((4, rows, 128), F32), pltpu.VMEM((4, rows, 128), jnp.int32),
            pltpu.VMEM((4, 3, rows, NT), F32), pltpu.VMEM((HC, cols), BF16), pltpu.VMEM((HC, cols), BF16),
            pltpu.VMEM((part, 4 * rows), BF16), pltpu.VMEM((4, rows, HC), F32), pltpu.VMEM((4, rows, HC), F32),
            pltpu.VMEM((chunks, 4, 2 * tok, HC), F32), pltpu.VMEM((ACCS, 4, 2 * tok, HC), F32),
            pltpu.VMEM((chunks, 2, tok, HC), F32), pltpu.VMEM((chunks, 4, tok, HC), F32),
            pltpu.VMEM((PH, PC), BF16), pltpu.VMEM((PH, PC), BF16), pltpu.VMEM((2 * tok, hid), BF16),
            dma((4,)), dma((2,)), dma((3,)), dma(()), dma((2,)), dma((chunks,)), dma((chunks,)),
            dma((chunks, 2)), dma((chunks, 2)), dma((chunks, 4)), dma((chunks, 4)), dma((2,)),
        ],
        compiler_params=pltpu.CompilerParams(collective_id=1, has_side_effects=True, vmem_limit_bytes=VMEM),
        name="grad_x_scatter",
    )(z, lcol, lab, w, xt)


def k3_kernel(g, xt, part, out, gv, xv, ob0, ob1, cb0, cb1, gsem, xsem, osem, isem, psem):
    prows, cols = part.shape
    hid = out.shape[0]
    rest = hid - prows
    blocks = cols // PC
    nb = rest // PH
    nc = prows // PH

    def g_load(c):
        return pltpu.make_async_copy(g.at[:, pl.ds(c * PC, PC)], gv.at[:, pl.ds(c * PC, PC)], gsem.at[c])

    cx = pltpu.make_async_copy(xt.at[pl.ds(prows, rest)], xv, xsem)
    cx.start()
    g_load(0).start()

    def tile(ref, r, c):
        return ref.at[pl.ds(r, PH), pl.ds(pl.multiple_of(c * PC, PC), PC)]

    def c_in(c, k, cb):
        return pltpu.make_async_copy(tile(part, k * PH, c), cb.at[k], isem.at[0 if cb is cb0 else 1, k])

    def c_out(c, k, cb):
        return pltpu.make_async_copy(cb.at[k], tile(out, k * PH, c), psem.at[0 if cb is cb0 else 1, k])

    def o_copy(c, k, ob):
        return pltpu.make_async_copy(ob.at[k], tile(out, prows + k * PH, c), osem.at[0 if ob is ob0 else 1, k])

    for k in range(nc):
        c_in(0, k, cb0).start()
    for c in range(1, blocks):
        g_load(c).start()
    cx.wait()

    def half(c, ob, cb, other):
        pltpu.make_async_copy(g.at[:, pl.ds(0, PC)], gv.at[:, pl.ds(0, PC)], gsem.at[c]).wait()

        @pl.when(c >= 2)
        def _():
            for k in range(nb):
                o_copy(c - 2, k, ob).wait()

        gs = pl.ds(pl.multiple_of(c * PC, PC), PC)
        for k in range(nb):
            ob[k] = jnp.dot(xv[k * PH:(k + 1) * PH], gv[:, gs], preferred_element_type=F32).astype(BF16)
        for k in range(nb):
            o_copy(c, k, ob).start()
        for k in range(nc):
            c_in(c, k, cb).wait()
            c_out(c, k, cb).start()

        @pl.when(c >= 1)
        def _():
            for k in range(nc):
                c_out(c - 1, k, other).wait()

        @pl.when(c + 1 < blocks)
        def _():
            for k in range(nc):
                c_in(c + 1, k, other).start()

    def step(i, _):
        half(2 * i, ob0, cb0, cb1)
        half(2 * i + 1, ob1, cb1, cb0)
        return 0

    lax.fori_loop(0, blocks // 2, step, 0)
    for k in range(nc):
        c_out(blocks - 1, k, cb1).wait()
    for k in range(nb):
        o_copy(blocks - 2, k, ob0).wait()
        o_copy(blocks - 1, k, ob1).wait()


def k3(g, xt, part):
    hid = xt.shape[0]
    rows, cols = g.shape
    prows = part.shape[0]
    rest = hid - prows
    hbm = pl.BlockSpec(memory_space=pltpu.MemorySpace.HBM)
    dma = pltpu.SemaphoreType.DMA
    return pl.pallas_call(
        k3_kernel,
        out_shape=jax.ShapeDtypeStruct((hid, cols), BF16),
        in_specs=[hbm] * 3,
        out_specs=hbm,
        scratch_shapes=[
            pltpu.VMEM((rows, cols), BF16), pltpu.VMEM((rest, rows), BF16), pltpu.VMEM((rest // PH, PH, PC), BF16),
            pltpu.VMEM((rest // PH, PH, PC), BF16), pltpu.VMEM((prows // PH, PH, PC), BF16), pltpu.VMEM((prows // PH, PH, PC), BF16),
            dma((cols // PC,)), dma(()), dma((2, rest // PH)), dma((2, prows // PH)), dma((2, prows // PH)),
        ],
        compiler_params=pltpu.CompilerParams(vmem_limit_bytes=VMEM),
        name="grad_w_rest",
    )(g, xt, part)


def solution(mesh):
    n = mesh.shape["tp"]

    def local_step(x_a, x_b, labels_a, labels_b, w):
        z, xt, lcol, labrel, loss = k1(n, x_a, x_b, labels_a, labels_b, w)
        gxa, gxb, g, part = k2(n, 18, z, lcol, labrel, w, xt)
        return loss[0, :2], k3(g, xt, part), gxa, gxb

    row_spec = P(("dp", "tp"), None)
    label_spec = P(("dp", "tp"))
    return jax.shard_map(local_step, mesh=mesh, in_specs=(row_spec, row_spec, label_spec, label_spec, P(None, "tp")), out_specs=(P("dp"), P("dp", "tp"), row_spec, row_spec), check_vma=False)
```

time: 278 us -> 185 us (0.67)
  Pallas kernels: 0 us -> 180 us
  matrix products: 146 us -> 0 us
  waiting for transfers between devices: 46.1 us -> 0 us
  blocking collectives: 37.8 us -> 0 us
  other arithmetic: 32.8 us -> 0.75 us
  between operations: 14.1 us -> 0.68 us
    pallas_call x0 -> x3, Pallas kernels: none -> 180 us  [the longest x1 83.7 us: k2(): pl.pallas_call(functools.partial(k2_kernel, n, cover), out_shape=[jax.Sha...]
    dot_general x3 -> x0, matrix products: 146 us -> none  [the longest x1 51.1 us: local_step(): jnp.einsum('mth,mtv->hv', x_full, grad_logits, preferred_element_type=jnp...]
    all_gather x1 -> x0, waiting for transfers between devices: 29.8 us -> none  [local_step(): x_full = lax.all_gather(jnp.stack([x_a, x_b]), 'tp', axis=1, tiled=True)]
    reduce_scatter x1 -> x0, waiting for transfers between devices: 16.2 us -> none  [local_step(): lax.psum_scatter(grad_part, 'tp', scatter_dimension=1, tiled=True)]
    dot_general x1 -> x0, other arithmetic: 16.2 us -> none  [local_step(): jnp.einsum('mtv,hv->mth', grad_logits, w_local, preferred_element_type=jn...]
    psum x1 -> x0, blocking collectives: 13.5 us -> none  [local_step(): lax.psum(jnp.stack([jnp.sum(shifted, axis=-1), local_target]), 'tp')]
    all_gather x1 -> x0, blocking collectives: 12.3 us -> none  [local_step(): lax.all_gather(jnp.stack([labels_a, labels_b]), 'tp', axis=1, tiled=True)]
    pmax x1 -> x0, blocking collectives: 12 us -> none  [local_step(): row_max = lax.pmax(jnp.max(logits, axis=-1), 'tp')]
  transfers between devices with their start and end apart: 2 -> 0, of which waited for: 2 -> 0; matrix products, arithmetic and copies ran while one was open for 19% -> 0% of each run, Pallas kernels for 0% -> 0%
where the time goes in v1:
time: 185 us
  Pallas kernels  180 us (97%)
  local copies, waits for them, and re-layouts  3.29 us (2%)
    pallas_call x1, Pallas kernels, k2(): pl.pallas_call(functools.partial(k2_kernel, n, cover), out_shape=[jax.Sha...  83.7 us
    pallas_call x1, Pallas kernels, k1(): pl.pallas_call(functools.partial(k1_kernel, n), out_shape=[jax.ShapeDtype...  65.7 us
    pallas_call x1, Pallas kernels, k3(): pl.pallas_call(k3_kernel, out_shape=jax.ShapeDtypeStruct((hid, cols), BF1...  30.5 us

profile of v1, /device:TPU:81, one launch (start us, length us, event | category | flops | bytes accessed | tf_op | source)
XLA Modules:
  0.0 184.5 jit_solution(12171847802502406538)
XLA Ops:
  0.6 0.7 pad_add_fusion
  1.4 0.6 broadcast_in_dim.2.lab
  2.0 65.7 %gather_logits.1 = (f32[4,2,6,256,512]{4,3,2,1,0:T(8,128)}, bf16[3072,1024]{1,0:T(8,128)(2,1)}, f32[4,256,128]{2,1,0:T(8,128)}, s32[4,256,128]{2,1,0:T(8,128)}, f32[8,128]{1,0:T(8,128)}) custom-call(bf16[64,3072]{1,0:T(8,128)(2,1)} %xa.1, bf16[64,3072]{1,0:T(8,128)(2,1)} %xb.1, s32[8,128]{1,0:T(8,128)} %broadcast_in_dim.2.lab, bf16[3072,6144]{1,0:T(8,128)(2,1)} %w.3), custom_call_target="tpu_custom_call" | custom-call | tf_op jit(solution)/shard_map/gather_logits/pallas_call | solution.py:278
  67.7 1.2 slice_bitcast_fusion
  68.9 83.7 %grad_x_scatter.1 = (bf16[64,3072]{1,0:T(8,128)(2,1)}, bf16[64,3072]{1,0:T(8,128)(2,1)}, bf16[1024,6144]{1,0:T(8,128)(2,1)}, bf16[1536,6144]{1,0:T(8,128)(2,1)}) custom-call(f32[4,2,6,256,512]{4,3,2,1,0:T(8,128)} %get-tuple-element.14.z, f32[4,256,128]{2,1,0:T(8,128)} %get-tuple-element.15.lcol, s32[4,256,128]{2,1,0:T(8,128)} %get-tuple-element.16.lab, ...), custom_call_target="tpu_custom_call" | custom-call | tf_op jit(solution)/shard_map/grad_x_scatter/pallas_call | solution.py:506
  152.5 0.0 copy-start.1
  152.5 0.0 copy-start
  152.5 30.5 %grad_w_rest.1 = bf16[3072,6144]{1,0:T(8,128)(2,1)} custom-call(bf16[1024,6144]{1,0:T(8,128)(2,1)} %get-tuple-element.18.g, bf16[3072,1024]{1,0:T(8,128)(2,1)} %get-tuple-element.17.xt, bf16[1536,6144]{1,0:T(8,128)(2,1)} %get-tuple-element.19.part), custom_call_target="tpu_custom_call" | custom-call | tf_op jit(solution)/shard_map/grad_w_rest/pallas_call | solution.py:607
  183.0 0.0 copy-done.1
  183.0 0.7 copy.11
  183.8 0.0 copy-done
  183.8 0.7 copy.12
Async XLA Ops:
  152.5 30.5 %copy-start.1 = (bf16[64,3072]{1,0:T(8,128)(2,1)S(1)}, bf16[64,3072]{1,0:T(8,128)(2,1)}, u32[]{:S(2)}) copy-start(bf16[64,3072]{1,0:T(8,128)(2,1)} %get-tuple-element.28) | copy-start | bytes 1179652
  152.5 31.3 %copy-start = (bf16[64,3072]{1,0:T(8,128)(2,1)S(1)}, bf16[64,3072]{1,0:T(8,128)(2,1)}, u32[]{:S(2)}) copy-start(bf16[64,3072]{1,0:T(8,128)(2,1)} %get-tuple-element.29) | copy-start | bytes 1179652

commit v2 on v1

--- a/solution.py
+++ b/solution.py
@@ -1,3 +1,4 @@
+import math
 import functools
 import jax
 import jax.numpy as jnp
@@ -129,12 +130,14 @@
                 epilogue(zb.at[t - 1], (q * NS + t - 1) * NT)
             elif q:
                 epilogue(zprev.at[NS - 1], (NS - 1) * NT)
+            if q and t == NS // 2:
+                for ev, fn in enumerate(late):
+                    pl.when(g == ev)(fn)
             zb[t] = jnp.dot(xc[...], ws[:, (q * NS + t) * NT:(q * NS + t + 1) * NT], preferred_element_type=F32)
 
     def step(g, _):
-        for ev, fn in events.items():
-            if ev % 2 == 0:
-                pl.when(g == ev // 2)(fn)
+        for ev, fn in enumerate(early):
+            pl.when(g == ev + 1)(fn)
         xc[...] = xs[g]
         lc[...] = labrel[g]
         mc[...] = jnp.full((rows, 128), LOW, F32)
@@ -150,9 +153,6 @@
             z_copy(g - 1, zb0).wait()
 
         half_step(g, 0, zb0, zb1)
-        for ev, fn in events.items():
-            if ev % 2 == 1:
-                pl.when(g == ev // 2)(fn)
 
         @pl.when(g == 0)
         def _():
@@ -199,7 +199,7 @@
     def ev_f2():
         c_d[3].wait_recv()
 
-    events = {1: ev_a, 2: ev_a2, 3: ev_b, 4: ev_b2, 5: ev_f, 6: ev_f2}
+    late, early = (ev_a, ev_b, ev_f), (ev_a2, ev_b2, ev_f2)
     lax.fori_loop(0, 4, step, 0)
 
     def rows_of(ref, r, f):
@@ -287,7 +287,7 @@
             pltpu.VMEM((NS, rows, NT), F32), pltpu.VMEM((NS, rows, NT), F32), pltpu.VMEM((rows, 128), F32), pltpu.VMEM((rows, 128), F32), pltpu.VMEM((rows, 128), F32), pltpu.VMEM((rows, 128), jnp.int32), pltpu.VMEM((4, rows, 128), F32), pltpu.VMEM((4, rows, 128), F32),
             pltpu.VMEM((4, rows, 128), F32), pltpu.VMEM((n, 8, 2 * tok), jnp.int32), pltpu.VMEM((4, rows, 128), jnp.int32),
             pltpu.VMEM((3, n, 2 * tok), F32), pltpu.VMEM((n, 3, n, 2 * tok), F32), pltpu.VMEM((n, 2 * tok), F32), pltpu.VMEM((8, 128), F32),
-            pltpu.SemaphoreType.DMA((tiles // NS,)), pltpu.SemaphoreType.DMA((2,)), pltpu.SemaphoreType.DMA((4,)),
+            pltpu.SemaphoreType.DMA((2,)), pltpu.SemaphoreType.DMA((2,)), pltpu.SemaphoreType.DMA((4,)),
             pltpu.SemaphoreType.DMA((12,)), pltpu.SemaphoreType.DMA((12,)), pltpu.SemaphoreType.DMA((n,)), pltpu.SemaphoreType.DMA((n,)),
             pltpu.SemaphoreType.DMA((n,)), pltpu.SemaphoreType.DMA((n,)),
         ],
@@ -301,7 +301,7 @@
 PH, PC = 512, 1024
 
 
-def k2_kernel(n, cover, z, lcol, lab, w, xt, dxa_out, dxb_out, g_out, dw_out,
+def k2_kernel(n, cover, z, lcol, lab, w, xt, dx_out, g_out, dw_out,
               g, lv, bv, z4, w0, w1, xv, d0, d1, pr, acc, r1, r2, ob0, ob1, oa,
               zsem, wsem, lsem, gsem, osem, psend, precv, s1send, s1recv, s2send, s2recv, fsem):
     me = lax.axis_index("tp")
@@ -336,7 +336,7 @@
     small[2].start()
     small[0].wait()
     small[1].wait()
-    inv = 1.0 / (tok * n)
+    inv, log_t = 1.0 / (tok * n), math.log(tok * n)
 
     def soft(i, _):
         slot = lax.rem(i, 4)
@@ -349,13 +349,13 @@
         gi, rest = i // (halves * sub // 3), lax.rem(i, halves * sub // 3)
         for r0 in range(0, rows, 32):
             rs = pl.ds(r0, 32)
-            lse = lv[gi, rs]
+            lse = lv[gi, rs] + log_t
             lr = bv[gi, rs] - rest * (3 * NT)
             for t in range(3):
                 out = []
                 for k in range(NT // 128):
                     p = jnp.exp(z4[slot, t, rs, k * 128:(k + 1) * 128] - lse)
-                    out.append((jnp.where(lr == t * NT + k * 128, p - 1.0, p) * inv).astype(BF16))
+                    out.append(jnp.where(lr == t * NT + k * 128, p - inv, p).astype(BF16))
                 g[pl.ds(pl.multiple_of(gi * rows + r0, 32), 32), pl.ds(pl.multiple_of(rest * (3 * NT) + t * NT, NT), NT)] = jnp.concatenate(out, axis=1)
         return 0
 
@@ -483,16 +483,14 @@
 
     lax.fori_loop(0, cover // 2 - chunks, two, 0)
     do_last(end)
-    outs = [pltpu.make_async_copy(oa.at[lo], dxa_out, fsem.at[0]), pltpu.make_async_copy(oa.at[hi], dxb_out, fsem.at[1])]
-    for c in outs:
-        c.start()
+    c_dx = pltpu.make_async_copy(oa, dx_out, fsem)
+    c_dx.start()
     pair(chunks - 2, d0).wait_send()
     pair(chunks - 1, d1).wait_send()
     dw_copy(cover - 2, ob0).wait()
     dw_copy(cover - 1, ob1).wait()
     c_g.wait()
-    for c in outs:
-        c.wait()
+    c_dx.wait()
 
 
 def k2(n, cover, z, lcol, lab, w, xt):
@@ -505,10 +503,10 @@
     dma = pltpu.SemaphoreType.DMA
     return pl.pallas_call(
         functools.partial(k2_kernel, n, cover),
-        out_shape=[jax.ShapeDtypeStruct((tok, hid), BF16), jax.ShapeDtypeStruct((tok, hid), BF16),
+        out_shape=[jax.ShapeDtypeStruct((2 * tok, hid), BF16),
                    jax.ShapeDtypeStruct((4 * rows, cols), BF16), jax.ShapeDtypeStruct((part, cols), BF16)],
         in_specs=[hbm] * 5,
-        out_specs=[hbm] * 4,
+        out_specs=[hbm] * 3,
         scratch_shapes=[
             pltpu.VMEM((4 * rows, cols), BF16), pltpu.VMEM((4, rows, 128), F32), pltpu.VMEM((4, rows, 128), jnp.int32),
             pltpu.VMEM((4, 3, rows, NT), F32), pltpu.VMEM((HC, cols), BF16), pltpu.VMEM((HC, cols), BF16),
@@ -517,14 +515,14 @@
             pltpu.VMEM((chunks, 2, tok, HC), F32), pltpu.VMEM((chunks, 4, tok, HC), F32),
             pltpu.VMEM((PH, PC), BF16), pltpu.VMEM((PH, PC), BF16), pltpu.VMEM((2 * tok, hid), BF16),
             dma((4,)), dma((2,)), dma((3,)), dma(()), dma((2,)), dma((chunks,)), dma((chunks,)),
-            dma((chunks, 2)), dma((chunks, 2)), dma((chunks, 4)), dma((chunks, 4)), dma((2,)),
+            dma((chunks, 2)), dma((chunks, 2)), dma((chunks, 4)), dma((chunks, 4)), dma(()),
         ],
         compiler_params=pltpu.CompilerParams(collective_id=1, has_side_effects=True, vmem_limit_bytes=VMEM),
         name="grad_x_scatter",
     )(z, lcol, lab, w, xt)
 
 
-def k3_kernel(g, xt, part, out, gv, xv, ob0, ob1, cb0, cb1, gsem, xsem, osem, isem, psem):
+def k3_kernel(g, xt, part, dx, loss, loss_out, out, dxa_out, dxb_out, dxv, dsem, gv, xv, ob0, ob1, cb0, cb1, gsem, xsem, osem, isem, psem):
     prows, cols = part.shape
     hid = out.shape[0]
     rest = hid - prows
@@ -535,6 +533,11 @@
     def g_load(c):
         return pltpu.make_async_copy(g.at[:, pl.ds(c * PC, PC)], gv.at[:, pl.ds(c * PC, PC)], gsem.at[c])
 
+    loss_out[0] = loss[0, 0]
+    loss_out[1] = loss[0, 1]
+    tok = dxa_out.shape[0]
+    c_dx = pltpu.make_async_copy(dx, dxv, dsem.at[0])
+    d_out = [pltpu.make_async_copy(dxv.at[pl.ds(i * tok, tok)], o, dsem.at[1 + i]) for i, o in enumerate((dxa_out, dxb_out))]
     cx = pltpu.make_async_copy(xt.at[pl.ds(prows, rest)], xv, xsem)
     cx.start()
     g_load(0).start()
@@ -555,6 +558,7 @@
         c_in(0, k, cb0).start()
     for c in range(1, blocks):
         g_load(c).start()
+    c_dx.start()
     cx.wait()
 
     def half(c, ob, cb, other):
@@ -585,6 +589,12 @@
                 c_in(c + 1, k, other).start()
 
     def step(i, _):
+        @pl.when(i == 1)
+        def _():
+            c_dx.wait()
+            for c in d_out:
+                c.start()
+
         half(2 * i, ob0, cb0, cb1)
         half(2 * i + 1, ob1, cb1, cb0)
         return 0
@@ -595,9 +605,11 @@
     for k in range(nb):
         o_copy(blocks - 2, k, ob0).wait()
         o_copy(blocks - 1, k, ob1).wait()
-
-
-def k3(g, xt, part):
+    for c in d_out:
+        c.wait()
+
+
+def k3(g, xt, part, dx, loss):
     hid = xt.shape[0]
     rows, cols = g.shape
     prows = part.shape[0]
@@ -606,17 +618,18 @@
     dma = pltpu.SemaphoreType.DMA
     return pl.pallas_call(
         k3_kernel,
-        out_shape=jax.ShapeDtypeStruct((hid, cols), BF16),
-        in_specs=[hbm] * 3,
-        out_specs=hbm,
+        out_shape=[jax.ShapeDtypeStruct((2,), F32), jax.ShapeDtypeStruct((hid, cols), BF16)] + [jax.ShapeDtypeStruct((dx.shape[0] // 2, hid), BF16)] * 2,
+        in_specs=[hbm] * 4 + [pl.BlockSpec(memory_space=pltpu.VMEM)],
+        out_specs=[pl.BlockSpec(memory_space=pltpu.SMEM)] + [hbm] * 3,
         scratch_shapes=[
+            pltpu.VMEM(dx.shape, BF16), dma((3,)),
             pltpu.VMEM((rows, cols), BF16), pltpu.VMEM((rest, rows), BF16), pltpu.VMEM((rest // PH, PH, PC), BF16),
             pltpu.VMEM((rest // PH, PH, PC), BF16), pltpu.VMEM((prows // PH, PH, PC), BF16), pltpu.VMEM((prows // PH, PH, PC), BF16),
             dma((cols // PC,)), dma(()), dma((2, rest // PH)), dma((2, prows // PH)), dma((2, prows // PH)),
         ],
         compiler_params=pltpu.CompilerParams(vmem_limit_bytes=VMEM),
         name="grad_w_rest",
-    )(g, xt, part)
+    )(g, xt, part, dx, loss)
 
 
 def solution(mesh):
@@ -624,8 +637,8 @@
 
     def local_step(x_a, x_b, labels_a, labels_b, w):
         z, xt, lcol, labrel, loss = k1(n, x_a, x_b, labels_a, labels_b, w)
-        gxa, gxb, g, part = k2(n, 18, z, lcol, labrel, w, xt)
-        return loss[0, :2], k3(g, xt, part), gxa, gxb
+        dx, g, part = k2(n, 18, z, lcol, labrel, w, xt)
+        return tuple(k3(g, xt, part, dx, loss))
 
     row_spec = P(("dp", "tp"), None)
     label_spec = P(("dp", "tp"))

time: 185 us -> 183 us (0.989)
  local copies, waits for them, and re-layouts: 3.29 us -> 0.6 us
where the time goes in v2:
time: 183 us
  Pallas kernels  181 us (99%)
    pallas_call x1, Pallas kernels, k2(): pl.pallas_call(functools.partial(k2_kernel, n, cover), out_shape=[jax.Sha...  83.1 us
    pallas_call x1, Pallas kernels, k1(): pl.pallas_call(functools.partial(k1_kernel, n), out_shape=[jax.ShapeDtype...  65.6 us
    pallas_call x1, Pallas kernels, k3(): pl.pallas_call(k3_kernel, out_shape=[jax.ShapeDtypeStruct((2,), F32), jax...  31.8 us

profile of v2, /device:TPU:81, one launch (start us, length us, event | category | flops | bytes accessed | tf_op | source)
XLA Modules:
  0.0 182.7 jit_solution(4971300609603604030)
XLA Ops:
  0.6 0.7 pad_add_fusion
  1.4 0.6 broadcast_in_dim.2.lab
  2.0 65.6 %gather_logits.1 = (f32[4,2,6,256,512]{4,3,2,1,0:T(8,128)}, bf16[3072,1024]{1,0:T(8,128)(2,1)}, f32[4,256,128]{2,1,0:T(8,128)}, s32[4,256,128]{2,1,0:T(8,128)}, f32[8,128]{1,0:T(8,128)}) custom-call(bf16[64,3072]{1,0:T(8,128)(2,1)} %xa.1, bf16[64,3072]{1,0:T(8,128)(2,1)} %xb.1, s32[8,128]{1,0:T(8,128)} %broadcast_in_dim.2.lab, bf16[3072,6144]{1,0:T(8,128)(2,1)} %w.3), custom_call_target="tpu_custom_call" | custom-call | tf_op jit(solution)/shard_map/gather_logits/pallas_call | solution.py:278
  67.6 83.1 %grad_x_scatter.1 = (bf16[128,3072]{1,0:T(8,128)(2,1)}, bf16[1024,6144]{1,0:T(8,128)(2,1)}, bf16[1536,6144]{1,0:T(8,128)(2,1)}) custom-call(f32[4,2,6,256,512]{4,3,2,1,0:T(8,128)} %get-tuple-element.12.z, f32[4,256,128]{2,1,0:T(8,128)} %get-tuple-element.13.lcol, s32[4,256,128]{2,1,0:T(8,128)} %get-tuple-element.14.lab, bf16[3072,6144]{1,0:T(8,128)(2,1)} %w.3, ...), custom_call_target="tpu_custom_call" | custom-call | tf_op jit(solution)/shard_map/grad_x_scatter/pallas_call | solution.py:504
  150.7 31.8 %grad_w_rest.1 = (f32[2]{0:T(128)}, bf16[3072,6144]{1,0:T(8,128)(2,1)}, bf16[64,3072]{1,0:T(8,128)(2,1)}, bf16[64,3072]{1,0:T(8,128)(2,1)}) custom-call(bf16[1024,6144]{1,0:T(8,128)(2,1)} %get-tuple-element.16.g, bf16[3072,1024]{1,0:T(8,128)(2,1)} %get-tuple-element.15.xt, bf16[1536,6144]{1,0:T(8,128)(2,1)} %get-tuple-element.17.part, ...), custom_call_target="tpu_custom_call" | custom-call | tf_op jit(solution)/shard_map/grad_w_rest/pallas_call | solution.py:619
